TPU v7x, 32 devices: a whole 2x2x4 slice. The times are simulated.
32 devices in a mesh: sims: 2 (over x), rows: 4 (over y, core), fields: 4 (over z).
Axes of the slice: x: 2, y: 2, z: 4, core: 2. Of those that a mesh axis runs over, the one named last changes fastest.
Arguments:
- sky_maps: float32 [6, 32, 16384], P('sims', 'rows', 'fields'), parts along dimension 0, may hold values from -7 to 7
- band_cuts: int32 [6], replicated, may hold values from 1 to 8191, as said below
- filters: float32 [3, 32, 16384], P(None, ('rows', 'fields')), may hold values from 0.3 to 3
- wiener: float32 [2, 32, 16384], P(None, ('rows', 'fields')), may hold values from 0.3 to 3
- response: float32 [32, 16384], P(('rows', 'fields')), may hold values from 0.5 to 2
Outputs:
- phi_curl: float32 [4, 32, 16384], P('sims', 'rows', 'fields'), parts along dimension 0
There are 2 independent parts, one for each index of `sims`. A program takes and returns all parts, laid end to end along the dimension named above; an argument that names none is the same for every part. Nothing has to cross between parts.
Inputs may be any that keep to these rules, and one draw needn't show every extreme that they name: `band_cuts`: entries 0, 2 and 4 are the smallest multipole indices of the temperature, polarization and estimate bands and lie below 512; entries 1, 3 and 5 are the largest and are at least 4096.
All inputs are finite; a program needn't handle non-finite values.
Results may differ from a plain program's by a relative error of at most 0.00019.
Values sent between devices are 32-bit elements; how exact they have to be, the bound alone decides.
No kernel may reach another device: no remote copies, remote signals or barrier semaphores. Data moves between devices by JAX's collectives and lax.ppermute only.
A program may use at most 128 MiB of HBM per device.

v0:
```python
import math

import jax
import jax.numpy as jnp
from jax import lax
from jax.sharding import PartitionSpec as P

NC = 16384


exact_mode = lax.Precision.HIGHEST


def split_factor(length):
    best_first = 1
    for divisor in range(1, math.isqrt(length) + 1):
        if length % divisor == 0:
            best_first = divisor
    return (best_first, length // best_first)


def phase_table(left_index, right_index, period, direction):
    product = left_index[:, None] * right_index[None, :] % period
    angles = direction * 2.0 * math.pi / period * product.astype(jnp.float32)
    return (jnp.cos(angles), jnp.sin(angles))


def complex_einsum(formula, data_pair, table_pair):
    data_real, data_imag = data_pair
    table_real, table_imag = table_pair
    real_out = jnp.einsum(formula, data_real, table_real, precision=exact_mode)
    imag_out = jnp.einsum(formula, data_real, table_imag, precision=exact_mode)
    if data_imag is not None:
        real_out = real_out - jnp.einsum(formula, data_imag, table_imag, precision=exact_mode)
        imag_out = imag_out + jnp.einsum(formula, data_imag, table_real, precision=exact_mode)
    return (real_out, imag_out)


def complex_mul(left_pair, right_pair):
    return (
        left_pair[0] * right_pair[0] - left_pair[1] * right_pair[1],
        left_pair[0] * right_pair[1] + left_pair[1] * right_pair[0],
    )


def conj_mul(left_pair, right_pair):
    return (
        left_pair[0] * right_pair[0] + left_pair[1] * right_pair[1],
        left_pair[0] * right_pair[1] - left_pair[1] * right_pair[0],
    )


def row_transform(data_pair, direction):
    batch_len, length, block_width = data_pair[0].shape
    outer_len, inner_len = split_factor(length)
    outer_ids = jnp.arange(outer_len, dtype=jnp.int32)
    inner_ids = jnp.arange(inner_len, dtype=jnp.int32)
    real_in = data_pair[0].reshape(batch_len, outer_len, inner_len, block_width)
    imag_in = None
    if data_pair[1] is not None:
        imag_in = data_pair[1].reshape(batch_len, outer_len, inner_len, block_width)
    middle = complex_einsum(
        "bjmc,jk->bkmc", (real_in, imag_in), phase_table(outer_ids, outer_ids, outer_len, direction)
    )
    twiddle = phase_table(outer_ids, inner_ids, length, direction)
    middle = complex_mul(middle, (twiddle[0][None, :, :, None], twiddle[1][None, :, :, None]))
    result = complex_einsum(
        "bkmc,mq->bqkc", middle, phase_table(inner_ids, inner_ids, inner_len, direction)
    )
    norm_factor = 1.0 if direction < 0 else 1.0 / length
    return (
        result[0].reshape(batch_len, length, block_width) * norm_factor,
        result[1].reshape(batch_len, length, block_width) * norm_factor,
    )


def block_order(groups, fields_count):
    positions = jnp.arange(groups, dtype=jnp.int32)
    blocks = positions % fields_count * (groups // fields_count) + positions // fields_count
    return (positions, blocks)


def column_forward(data_pair, groups, fields_count):
    batch_len, local_rows, total_len = data_pair[0].shape
    block_width = total_len // groups
    positions, blocks = block_order(groups, fields_count)
    column_ids = jnp.arange(block_width, dtype=jnp.int32)
    shaped = (
        data_pair[0].reshape(batch_len, local_rows, groups, block_width),
        data_pair[1].reshape(batch_len, local_rows, groups, block_width),
    )
    middle = complex_einsum("brpc,pk->brkc", shaped, phase_table(blocks, positions, groups, -1.0))
    twiddle = phase_table(positions, column_ids, total_len, -1.0)
    middle = complex_mul(middle, (twiddle[0][None, None], twiddle[1][None, None]))
    result = complex_einsum(
        "brkc,cq->brqk", middle, phase_table(column_ids, column_ids, block_width, -1.0)
    )
    return (
        result[0].reshape(batch_len, local_rows, total_len),
        result[1].reshape(batch_len, local_rows, total_len),
    )


def column_inverse(data_pair, groups, fields_count):
    batch_len, local_rows, total_len = data_pair[0].shape
    block_width = total_len // groups
    positions, blocks = block_order(groups, fields_count)
    column_ids = jnp.arange(block_width, dtype=jnp.int32)
    shaped = (
        data_pair[0].reshape(batch_len, local_rows, block_width, groups),
        data_pair[1].reshape(batch_len, local_rows, block_width, groups),
    )
    middle = complex_einsum(
        "brqk,qc->brkc", shaped, phase_table(column_ids, column_ids, block_width, 1.0)
    )
    twiddle = phase_table(positions, column_ids, total_len, 1.0)
    middle = complex_mul(middle, (twiddle[0][None, None], twiddle[1][None, None]))
    result = complex_einsum("brkc,kp->brpc", middle, phase_table(positions, blocks, groups, 1.0))
    norm_factor = 1.0 / total_len
    return (
        result[0].reshape(batch_len, local_rows, total_len) * norm_factor,
        result[1].reshape(batch_len, local_rows, total_len) * norm_factor,
    )


def body(sky_maps, band_cuts, filters, wiener, response):
    rows_count = lax.axis_size("rows")
    fields_count = lax.axis_size("fields")
    groups = rows_count * fields_count
    local_rows = filters.shape[1]
    total_rows = local_rows * groups
    row_ratio = NC // total_rows

    def forward_columns(stacked):
        return jnp.stack(column_forward((stacked[0], stacked[1]), groups, fields_count))

    def inverse_rows(stacked):
        return jnp.stack(row_transform((stacked[0], stacked[1]), 1.0))

    def inverse_columns(stacked):
        return jnp.stack(column_inverse((stacked[0], stacked[1]), groups, fields_count))

    def to_frequency(stacked):
        batch_len = stacked.shape[1]
        block_width = stacked.shape[3]
        shaped = stacked.reshape(
            2, batch_len, rows_count, fields_count, local_rows, 1, 1, block_width
        )
        arrived = lax.all_to_all(
            lax.all_to_all(shaped, "rows", split_axis=2, concat_axis=5, tiled=True),
            "fields",
            split_axis=3,
            concat_axis=6,
            tiled=True,
        )
        result = forward_columns(arrived.reshape(2, batch_len, local_rows, groups * block_width))
        return result

    def to_space(stacked):
        batch_len = stacked.shape[1]
        block_width = stacked.shape[3] // groups
        shaped = stacked.reshape(
            2, batch_len, 1, 1, local_rows, rows_count, fields_count, block_width
        )
        arrived = lax.all_to_all(
            lax.all_to_all(shaped, "rows", split_axis=5, concat_axis=2, tiled=True),
            "fields",
            split_axis=6,
            concat_axis=3,
            tiled=True,
        )
        result = inverse_rows(arrived.reshape(2, batch_len, total_rows, block_width))
        return result

    slab_spectra = jnp.stack(
        row_transform(
            (lax.all_to_all(sky_maps, "rows", split_axis=2, concat_axis=1, tiled=True), None), -1.0
        )
    )
    sky_spectra = to_frequency(slab_spectra)
    row_ids = lax.axis_index(("rows", "fields")) * local_rows + jnp.arange(
        local_rows, dtype=jnp.int32
    )
    freq_rows = jnp.where(row_ids < total_rows // 2, row_ids, row_ids - total_rows)[:, None]
    column_ids = jnp.arange(NC, dtype=jnp.int32)
    freq_cols = jnp.where(column_ids < NC // 2, column_ids, column_ids - NC)[None, :]
    scaled_rows = row_ratio * freq_rows
    radius_sq = freq_cols * freq_cols + scaled_rows * scaled_rows

    def band_mask(lower_cut, upper_cut):
        inside = (radius_sq >= lower_cut * lower_cut) & (radius_sq <= upper_cut * upper_cut)
        return inside.astype(jnp.float32)

    mask_temp = band_mask(band_cuts[0], band_cuts[1])
    mask_pol = band_mask(band_cuts[2], band_cuts[3])
    mask_out = band_mask(band_cuts[4], band_cuts[5])
    radius_floor = jnp.maximum(radius_sq, 1).astype(jnp.float32)
    cos_two = (freq_cols * freq_cols - scaled_rows * scaled_rows).astype(jnp.float32) / radius_floor
    sin_two = (2 * freq_cols * scaled_rows).astype(jnp.float32) / radius_floor
    along_x = (2 * freq_cols).astype(jnp.float32) / NC
    along_y = (2 * freq_rows).astype(jnp.float32) / total_rows
    raising = (-along_y + 0.0 * along_x, along_x + 0.0 * along_y)
    lowering = (along_y + 0.0 * along_x, along_x + 0.0 * along_y)
    rotation = (cos_two, sin_two)
    temp_modes = (sky_spectra[0, 0], sky_spectra[1, 0])
    stokes_q = (sky_spectra[0, 1], sky_spectra[1, 1])
    stokes_u = (sky_spectra[0, 2], sky_spectra[1, 2])
    e_modes = (
        -(cos_two * stokes_q[0] + sin_two * stokes_u[0]),
        -(cos_two * stokes_q[1] + sin_two * stokes_u[1]),
    )
    b_modes = (
        sin_two * stokes_q[0] - cos_two * stokes_u[0],
        sin_two * stokes_q[1] - cos_two * stokes_u[1],
    )
    temp_weight = mask_temp * filters[0]
    e_weight = mask_pol * filters[1]
    b_weight = mask_pol * filters[2]
    temp_bar = (temp_weight * temp_modes[0], temp_weight * temp_modes[1])
    e_bar = (e_weight * e_modes[0], e_weight * e_modes[1])
    b_bar = (b_weight * b_modes[0], b_weight * b_modes[1])
    grad_temp = complex_mul(raising, (wiener[0] * temp_bar[0], wiener[0] * temp_bar[1]))
    pol_sum = complex_mul((e_bar[0] - b_bar[1], e_bar[1] + b_bar[0]), rotation)
    pol_bar = (-pol_sum[0], -pol_sum[1])
    pol_rot = complex_mul((wiener[1] * e_bar[0], wiener[1] * e_bar[1]), rotation)
    pol_wiener = (-pol_rot[0], -pol_rot[1])
    spin_three = complex_mul(raising, pol_wiener)
    spin_one = complex_mul(lowering, pol_wiener)
    leg_spectra = jnp.stack(
        [
            jnp.stack([temp_bar[0], grad_temp[0], pol_bar[0], spin_three[0], spin_one[0]]),
            jnp.stack([temp_bar[1], grad_temp[1], pol_bar[1], spin_three[1], spin_one[1]]),
        ]
    )
    leg_maps = to_space(inverse_columns(leg_spectra))
    temp_leg = (leg_maps[0, 0], leg_maps[1, 0])
    grad_leg = (leg_maps[0, 1], leg_maps[1, 1])
    pol_leg = (leg_maps[0, 2], leg_maps[1, 2])
    three_leg = (leg_maps[0, 3], leg_maps[1, 3])
    one_leg = (leg_maps[0, 4], leg_maps[1, 4])
    temp_term = complex_mul(temp_leg, grad_leg)
    raise_term = conj_mul(pol_leg, three_leg)
    lower_term = conj_mul(one_leg, pol_leg)
    current = (
        temp_term[0] + 0.5 * (raise_term[0] + lower_term[0]),
        temp_term[1] + 0.5 * (raise_term[1] + lower_term[1]),
    )
    current_rows = jnp.stack(row_transform((current[0][None], current[1][None]), -1.0))
    current_modes = to_frequency(current_rows)
    out_weight = mask_out * response
    estimate_modes = complex_mul(
        lowering, (out_weight * current_modes[0, 0], out_weight * current_modes[1, 0])
    )
    estimate_stack = jnp.stack([estimate_modes[0][None], estimate_modes[1][None]])
    estimate_maps = to_space(inverse_columns(estimate_stack))
    slab_result = estimate_maps[:, 0]
    return lax.all_to_all(slab_result, "rows", split_axis=1, concat_axis=2, tiled=True)


def solution(mesh):
    placed = (
        P("sims", "rows", "fields"),
        P(),
        P(None, ("rows", "fields"), None),
        P(None, ("rows", "fields"), None),
        P(("rows", "fields"), None),
    )
    return jax.shard_map(
        body, mesh=mesh, in_specs=placed, out_specs=P("sims", "rows", "fields"), check_vma=False
    )
```

profile of v0, /device:TPU:0, one launch (start us, length us, event | category | flops | bytes accessed | tf_op | source)
XLA Modules:
  0.0 572.1 jit_solution(2138556085943826780)
XLA Ops:
  0.0 6.7 %copy.84 = f32[3,8,4096]{1,0,2:T(4,128)} copy(f32[3,8,4096]{2,1,0:T(8,128)} %param.5) | data formatting | bytes 786432 | tf_op args[0]
  6.7 7.5 %reshape.1834 = f32[4,1,24576]{2,1,0:T(1,128)} reshape(f32[4096,3,8]{2,1,0:T(4,128)} %bitcast.453) | data formatting | bytes 786432
  14.2 4.3 all-to-all-start
  18.5 7.4 %all-to-all-done = f32[4,1,24576]{2,1,0:T(1,128)S(1)} async-done(((f32[4,1,24576]{2,1,0:T(1,128)}), f32[4,1,24576]{2,1,0:T(1,128)S(1)}, u32[]{:S(2)}, u32[]{:S(2)}) %all-to-all-start) | async-done | bytes 393248 | tf_op jit(solution)/shard_map/all_to_all | solution.py:177
  28.1 8.7 %reshape.1835 = f32[4096,3,8]{2,1,0:T(4,128)} reshape(f32[4,24576]{1,0:T(4,128)S(1)} %reduce) | data formatting | bytes 786432
  36.9 6.9 %copy.170 = f32[3,8,4,1024]{3,2,1,0:T(4,128)S(1)} copy(f32[3,8,4,1024]{1,0,3,2:T(4,128)} %bitcast.452) | data formatting | bytes 786432 | tf_op jit(solution)/shard_map/all_to_all | solution.py:177
  50.1 14.0 %all_to_all.165 = f32[2,3,4,4,2,1,1,1024]{7,4,3,1,6,5,0,2:T(2,128)S(1)} all-to-all(f32[2,3,4,4,2,1,1,1024]{7,4,3,1,6,5,0,2:T(2,128)S(1)} %copy.92), channel_id=1, replica_groups=mesh['sims'=2,'rows'=4,'fields'=4] {'rows'}, dimensions={2} | all-to-all | bytes 1572864 | tf_op jit(solution)/shard_map/all_to_all | solution.py:150
  65.1 5.7 all-to-all-start.2
  78.8 11.8 %all-to-all-done.2 = f32[2,3,1,4,2,4,1,1024]{7,4,5,1,0,6,2,3:T(2,128)S(1)} async-done(((f32[2,3,1,4,2,4,1,1024]{7,4,5,1,0,6,2,3:T(2,128)}), f32[2,3,1,4,2,4,1,1024]{7,4,5,1,0,6,2,3:T(2,128)S(1)}, u32[]{:S(2)}, u32[]{:S(2)}) %all-to-all-start.2) | async-done | bytes 786464 | tf_op jit(solution)/shard_map/all_to_all | solution.py:149
  93.6 18.6 %fusion.24 = f32[1024,3,2,16]{0,3,2,1:T(8,128)S(1)} fusion(f32[16,3,2,1024]{3,0,2,1:T(8,128)S(1)} %convolution_add_fusion.3, f32[16,3,2,1024]{3,0,2,1:T(8,128)S(1)} %convolution_subtract_fusion.3, f32[16,1024]{1,0:T(8,128)S(1)} %get-tuple-element.50, f32[16,1024]{1,0:T(8,128)S(1)} %get-tuple-element.51), kind=kOutput, calls=%fused_computation.27 | convolution fusion | flops 1222934528 | bytes 1310720 | tf_op jit(solution)/shard_map/brkc,cq->brqk/dot_general | solution.py:31
  112.1 19.3 %fusion.22 = f32[1024,3,2,16]{0,3,2,1:T(8,128)} fusion(f32[16,3,2,1024]{3,0,2,1:T(8,128)S(1)} %convolution_add_fusion.3, f32[16,3,2,1024]{3,0,2,1:T(8,128)S(1)} %convolution_subtract_fusion.3, f32[16,1024]{1,0:T(8,128)S(1)} %get-tuple-element.50, f32[16,1024]{1,0:T(8,128)S(1)} %get-tuple-element.51), kind=kOutput, calls=%fused_computation.25 | convolution fusion | flops 1222934528 | bytes 1310720 | tf_op jit(solution)/shard_map/brkc,cq->brqk/dot_general | solution.py:35
  131.4 19.2 %fusion.88 = f32[3,2,1024,16]{2,3,1,0:T(8,128)} fusion(f32[1024,3,2,16]{0,3,2,1:T(8,128)S(1)} %fusion.24, f32[16,3,2,1024]{3,0,2,1:T(8,128)S(1)} %convolution_add_fusion.3, f32[16,3,2,1024]{3,0,2,1:T(8,128)S(1)} %convolution_subtract_fusion.3, f32[16,1024]{1,0:T(8,128)S(1)} %get-tuple-element.50, f32[16,1024]{1,0:T(8,128)S(1)} %get-tuple-element.51), kind=kOutput, calls=%fused_computation.84 | convolution fusion | flops 1223032832 | bytes 1703936 | tf_op jit(solution)/shard_map/brkc,cq->brqk/dot_general | solution.py:34
  155.0 20.8 %fusion.94 = f32[3,2,1024,16]{2,3,1,0:T(8,128)} fusion(f32[1024,3,2,16]{0,3,2,1:T(8,128)} %fusion.22, f32[16,3,2,1024]{3,0,2,1:T(8,128)} %copy-done.6, f32[16,3,2,1024]{3,0,2,1:T(8,128)} %copy-done.5, f32[16,1024]{1,0:T(8,128)} %copy-done.8, f32[16,1024]{1,0:T(8,128)} %copy-done.10), kind=kOutput, calls=%fused_computation.86 | convolution fusion | flops 1223032832 | bytes 1703936 | tf_op jit(solution)/shard_map/brkc,cq->brqk/dot_general | solution.py:32
  195.4 20.3 %fusion.16 = f32[5,2,16,1024]{3,2,1,0:T(8,128)} fusion(f32[5,2,1024,16]{2,3,1,0:T(8,128)} %constant_dynamic-update-slice_fusion), kind=kOutput, calls=%fused_computation.19 | convolution fusion | flops 2027945984 | bytes 1310720 | tf_op jit(solution)/shard_map/brqk,qc->brkc/dot_general | solution.py:31
  219.8 18.7 %fusion.14 = f32[5,2,16,1024]{3,2,1,0:T(8,128)S(1)} fusion(f32[5,2,1024,16]{2,3,1,0:T(8,128)S(1)} %constant_dynamic-update-slice_fusion.5), kind=kOutput, calls=%fused_computation.17 | convolution fusion | flops 2027945984 | bytes 1310720 | tf_op jit(solution)/shard_map/brqk,qc->brkc/dot_general | solution.py:35
  238.5 20.2 %fusion.77 = f32[5,2,16,1024]{3,2,1,0:T(8,128)S(1)} fusion(f32[5,2,16,1024]{3,2,1,0:T(8,128)S(1)} %copy-done.19, f32[5,2,1024,16]{2,3,1,0:T(8,128)} %copy-done.13), kind=kOutput, calls=%fused_computation.75 | convolution fusion | flops 2028109824 | bytes 1966080 | tf_op jit(solution)/shard_map/brqk,qc->brkc/dot_general | solution.py:34
  258.8 18.8 %fusion.80 = f32[5,2,16,1024]{3,2,1,0:T(8,128)S(1)} fusion(f32[5,2,16,1024]{3,2,1,0:T(8,128)S(1)} %fusion.14, f32[5,2,1024,16]{2,3,1,0:T(8,128)S(1)} %copy-done.12), kind=kOutput, calls=%fused_computation.76 | convolution fusion | flops 2028109824 | bytes 1966080 | tf_op jit(solution)/shard_map/brqk,qc->brkc/dot_general | solution.py:32
  281.6 19.7 %all_to_all.166 = f32[2,5,1,1,2,4,4,1024]{7,6,4,1,3,2,0,5:T(4,128)S(1)} all-to-all(f32[2,5,1,1,2,4,4,1024]{7,6,4,1,3,2,0,5:T(4,128)S(1)} %copy.171), channel_id=1, replica_groups=mesh['sims'=2,'rows'=4,'fields'=4] {'rows'}, dimensions={5} | all-to-all | bytes 2621440 | tf_op jit(solution)/shard_map/all_to_all | solution.py:166
  307.0 31.0 %all-to-all-done.4 = f32[2,5,4,1,2,1,4,1024]{7,2,4,1,0,5,3,6:T(4,128)S(1)} async-done(((f32[2,5,4,1,2,1,4,1024]{7,2,4,1,0,5,3,6:T(4,128)}), f32[2,5,4,1,2,1,4,1024]{7,2,4,1,0,5,3,6:T(4,128)S(1)}, u32[]{:S(2)}, u32[]{:S(2)}) %all-to-all-start.4) | async-done | bytes 1310752 | tf_op jit(solution)/shard_map/all_to_all | solution.py:165
  353.2 8.4 %all_to_all.167 = f32[2,1,4,4,2,1,1,1024]{7,4,3,6,5,1,0,2:T(2,128)S(1)} all-to-all(f32[2,1,4,4,2,1,1,1024]{7,4,3,6,5,1,0,2:T(2,128)S(1)} %copy.129), channel_id=1, replica_groups=mesh['sims'=2,'rows'=4,'fields'=4] {'rows'}, dimensions={2} | all-to-all | bytes 524288 | tf_op jit(solution)/shard_map/all_to_all | solution.py:150
  368.1 6.4 %all-to-all-done.6 = f32[2,1,1,4,2,4,1,1024]{7,4,5,0,6,2,1,3:T(2,128)S(1)} async-done(((f32[2,1,1,4,2,4,1,1024]{7,4,5,0,6,2,1,3:T(2,128)}), f32[2,1,1,4,2,4,1,1024]{7,4,5,0,6,2,1,3:T(2,128)S(1)}, u32[]{:S(2)}, u32[]{:S(2)}) %all-to-all-start.6) | async-done | bytes 262176 | tf_op jit(solution)/shard_map/all_to_all | solution.py:149
  376.1 18.3 %fusion.12 = f32[1024,2,16]{0,2,1:T(8,128)S(1)} fusion(f32[16,1,2,1024]{3,0,2,1:T(8,128)S(1)} %fusion.97, f32[16,1,2,1024]{3,0,2,1:T(8,128)S(1)} %fusion.98, f32[16,1024]{1,0:T(8,128)S(1)} %copy-done.9, f32[16,1024]{1,0:T(8,128)S(1)} %copy-done.11), kind=kOutput, calls=%fused_computation.15 | convolution fusion | flops 417431552 | bytes 524288 | tf_op jit(solution)/shard_map/brkc,cq->brqk/dot_general | solution.py:34
  394.4 18.3 %fusion.10 = f32[1024,2,16]{0,2,1:T(8,128)S(1)} fusion(f32[16,1,2,1024]{3,0,2,1:T(8,128)S(1)} %fusion.97, f32[16,1,2,1024]{3,0,2,1:T(8,128)S(1)} %fusion.98, f32[16,1024]{1,0:T(8,128)S(1)} %copy-done.9, f32[16,1024]{1,0:T(8,128)S(1)} %copy-done.11), kind=kOutput, calls=%fused_computation.13 | convolution fusion | flops 417431552 | bytes 524288 | tf_op jit(solution)/shard_map/brkc,cq->brqk/dot_general | solution.py:32
  412.8 18.4 %fusion.114 = f32[1,2,1024,16]{2,3,1,0:T(8,128)S(1)} fusion(f32[1024,2,16]{0,2,1:T(8,128)S(1)} %fusion.12, f32[16,1,2,1024]{3,0,2,1:T(8,128)S(1)} %fusion.97, f32[16,1,2,1024]{3,0,2,1:T(8,128)S(1)} %fusion.98, f32[16,1024]{1,0:T(8,128)S(1)} %copy-done.9, f32[16,1024]{1,0:T(8,128)S(1)} %copy-done.11), kind=kOutput, calls=%fused_computation.110 | convolution fusion | flops 417464320 | bytes 655360 | tf_op jit(solution)/shard_map/brkc,cq->brqk/dot_general | solution.py:31
  432.1 18.2 %fusion.120 = f32[1,2,1024,16]{2,3,1,0:T(8,128)S(1)} fusion(f32[1024,2,16]{0,2,1:T(8,128)S(1)} %fusion.10, f32[16,1,2,1024]{3,0,2,1:T(8,128)S(1)} %fusion.97, f32[16,1,2,1024]{3,0,2,1:T(8,128)S(1)} %fusion.98, f32[16,1024]{1,0:T(8,128)S(1)} %copy-done.9, f32[16,1024]{1,0:T(8,128)S(1)} %copy-done.11), kind=kOutput, calls=%fused_computation.112 | convolution fusion | flops 417464320 | bytes 655360 | tf_op jit(solution)/shard_map/brkc,cq->brqk/dot_general | solution.py:35
  452.0 21.4 %fusion.4 = f32[2,16,1024]{2,1,0:T(8,128)S(1)} fusion(f32[2,1024,16]{2,1,0:T(8,128)S(1)} %reshape.1797), kind=kOutput, calls=%fused_computation.7 | convolution fusion | flops 417333248 | bytes 262144 | tf_op jit(solution)/shard_map/brqk,qc->brkc/dot_general | solution.py:34
  473.8 21.2 %fusion.2 = f32[2,16,1024]{2,1,0:T(8,128)S(1)} fusion(f32[2,1024,16]{2,1,0:T(8,128)S(1)} %reshape.1796), kind=kOutput, calls=%fused_computation.5 | convolution fusion | flops 417333248 | bytes 262144 | tf_op jit(solution)/shard_map/brqk,qc->brkc/dot_general | solution.py:32
  494.9 21.5 %fusion.105 = f32[2,16,1024]{2,1,0:T(8,128)S(1)} fusion(f32[2,16,1024]{2,1,0:T(8,128)S(1)} %fusion.4, f32[2,1024,16]{2,1,0:T(8,128)S(1)} %reshape.1796), kind=kOutput, calls=%fused_computation.107 | convolution fusion | flops 417366016 | bytes 393216 | tf_op jit(solution)/shard_map/brqk,qc->brkc/dot_general | solution.py:31
  516.4 21.1 %fusion.108 = f32[2,16,1024]{2,1,0:T(8,128)S(1)} fusion(f32[2,16,1024]{2,1,0:T(8,128)S(1)} %fusion.2, f32[2,1024,16]{2,1,0:T(8,128)S(1)} %reshape.1797), kind=kOutput, calls=%fused_computation.108 | convolution fusion | flops 417366016 | bytes 393216 | tf_op jit(solution)/shard_map/brqk,qc->brkc/dot_general | solution.py:35
  539.2 8.4 %all_to_all.168 = f32[2,1,1,1,2,4,4,1024]{7,6,4,3,2,1,0,5:T(4,128)S(1)} all-to-all(f32[2,1,1,1,2,4,4,1024]{7,6,4,3,2,1,0,5:T(4,128)S(1)} %copy.172), channel_id=1, replica_groups=mesh['sims'=2,'rows'=4,'fields'=4] {'rows'}, dimensions={5} | all-to-all | bytes 524288 | tf_op jit(solution)/shard_map/all_to_all | solution.py:166
  547.7 11.3 %all_to_all.169 = f32[2,1,4,1,2,1,4,1024]{7,2,4,0,5,3,1,6:T(4,128)S(1)} all-to-all(f32[2,1,4,1,2,1,4,1024]{7,2,4,0,5,3,1,6:T(4,128)S(1)} %copy.141), channel_id=1, replica_groups=mesh['sims'=2,'rows'=4,'fields'=4] {'fields'}, dimensions={6} | all-to-all | bytes 524288 | tf_op jit(solution)/shard_map/all_to_all | solution.py:165
  562.7 8.4 %all_to_all.170 = f32[2,32,1024]{2,0,1:T(2,128)S(1)} all-to-all(f32[2,32,1024]{2,0,1:T(2,128)S(1)} %copy.148), channel_id=1, replica_groups=mesh['sims'=2,'rows'=4,'fields'=4] {'rows'}, dimensions={1} | all-to-all | bytes 524288 | tf_op jit(solution)/shard_map/all_to_all | solution.py:257
  (197 shorter events, 82.4 us)
Async XLA Ops:
  14.2 11.7 %all-to-all-start = ((f32[4,1,24576]{2,1,0:T(1,128)}), f32[4,1,24576]{2,1,0:T(1,128)S(1)}, u32[]{:S(2)}, u32[]{:S(2)}) async-start(f32[4,1,24576]{2,1,0:T(1,128)} %reshape.1834), calls=%async_computation | async-start | bytes 786432 | tf_op jit(solution)/shard_map/all_to_all | solution.py:177
  49.1 21.7 %copy-start.14 = (s32[6]{0:T(128)S(1)}, s32[6]{0:T(128)}, u32[]{:S(2)}) copy-start(s32[6]{0:T(128)} %param.6) | copy-start | bytes 76
  65.1 25.4 %all-to-all-start.2 = ((f32[2,3,1,4,2,4,1,1024]{7,4,5,1,0,6,2,3:T(2,128)}), f32[2,3,1,4,2,4,1,1024]{7,4,5,1,0,6,2,3:T(2,128)S(1)}, u32[]{:S(2)}, u32[]{:S(2)}) async-start(f32[2,3,1,4,2,4,1,1024]{7,4,5,1,0,6,2,3:T(2,128)} %copy.93), calls=%async_computation.2 | async-start | bytes 1572864 | tf_op jit(solution)/shard_map/all_to_all | solution.py:149
  78.4 53.0 %copy-start.8 = (f32[16,1024]{1,0:T(8,128)}, f32[16,1024]{1,0:T(8,128)S(1)}, u32[]{:S(2)}) copy-start(f32[16,1024]{1,0:T(8,128)S(1)} %get-tuple-element.50) | copy-start | bytes 196612
  78.4 53.0 %copy-start.10 = (f32[16,1024]{1,0:T(8,128)}, f32[16,1024]{1,0:T(8,128)S(1)}, u32[]{:S(2)}) copy-start(f32[16,1024]{1,0:T(8,128)S(1)} %get-tuple-element.51) | copy-start | bytes 196612
  78.7 107.7 %copy-start.2 = (s32[16384]{0:T(1024)}, s32[16384]{0:T(1024)S(1)}, u32[]{:S(2)}) copy-start(s32[16384]{0:T(1024)S(1)} %get-tuple-element.54) | copy-start | bytes 196612
  93.0 38.4 %copy-start.5 = (f32[16,3,2,1024]{3,0,2,1:T(8,128)}, f32[16,3,2,1024]{3,0,2,1:T(8,128)S(1)}, u32[]{:S(2)}) copy-start(f32[16,3,2,1024]{3,0,2,1:T(8,128)S(1)} %convolution_subtract_fusion.3) | copy-start | bytes 1179652
  93.6 37.8 %copy-start.6 = (f32[16,3,2,1024]{3,0,2,1:T(8,128)}, f32[16,3,2,1024]{3,0,2,1:T(8,128)S(1)}, u32[]{:S(2)}) copy-start(f32[16,3,2,1024]{3,0,2,1:T(8,128)S(1)} %convolution_add_fusion.3) | copy-start | bytes 1179652
  180.2 6.2 %copy-start = (f32[1,3,2,16384]{3,2,1,0:T(2,128)S(1)}, f32[1,3,2,16384]{3,2,1,0:T(2,128)}, u32[]{:S(2)}) copy-start(f32[1,3,2,16384]{3,2,1,0:T(2,128)} %stack_reshape.4) | copy-start | bytes 1179652
  180.2 6.2 %copy-start.1 = (f32[1,3,2,16384]{3,2,1,0:T(2,128)S(1)}, f32[1,3,2,16384]{3,2,1,0:T(2,128)}, u32[]{:S(2)}) copy-start(f32[1,3,2,16384]{3,2,1,0:T(2,128)} %stack_reshape.5) | copy-start | bytes 1179652
  180.2 6.3 %copy-start.15 = (s32[2]{0:T(128)S(1)}, s32[2]{0:T(128)}, u32[]{:S(2)}) copy-start(s32[2]{0:T(128)} %get-tuple-element.47) | copy-start | bytes 28
  180.2 6.3 %copy-start.18 = (s32[2]{0:T(128)S(1)}, s32[2]{0:T(128)}, u32[]{:S(2)}) copy-start(s32[2]{0:T(128)} %get-tuple-element.46) | copy-start | bytes 28
  184.8 4.4 copy-start.4
  218.9 0.8 copy-start.13
  219.8 18.7 %copy-start.19 = (f32[5,2,16,1024]{3,2,1,0:T(8,128)S(1)}, f32[5,2,16,1024]{3,2,1,0:T(8,128)}, u32[]{:S(2)}) copy-start(f32[5,2,16,1024]{3,2,1,0:T(8,128)} %fusion.16) | copy-start | bytes 1966084
  238.5 20.3 %copy-start.12 = (f32[5,2,1024,16]{2,3,1,0:T(8,128)S(1)}, f32[5,2,1024,16]{2,3,1,0:T(8,128)}, u32[]{:S(2)}) copy-start(f32[5,2,1024,16]{2,3,1,0:T(8,128)} %constant_dynamic-update-slice_fusion) | copy-start | bytes 1966084
  303.2 34.8 %all-to-all-start.4 = ((f32[2,5,4,1,2,1,4,1024]{7,2,4,1,0,5,3,6:T(4,128)}), f32[2,5,4,1,2,1,4,1024]{7,2,4,1,0,5,3,6:T(4,128)S(1)}, u32[]{:S(2)}, u32[]{:S(2)}) async-start(f32[2,5,4,1,2,1,4,1024]{7,2,4,1,0,5,3,6:T(4,128)} %copy.110), calls=%async_computation.4 | async-start | bytes 2621440 | tf_op jit(solution)/shard_map/all_to_all | solution.py:165
  350.8 25.3 %copy-start.9 = (f32[16,1024]{1,0:T(8,128)S(1)}, f32[16,1024]{1,0:T(8,128)}, u32[]{:S(2)}) copy-start(f32[16,1024]{1,0:T(8,128)} %copy-done.8) | copy-start | bytes 196612
  350.8 25.3 %copy-start.11 = (f32[16,1024]{1,0:T(8,128)S(1)}, f32[16,1024]{1,0:T(8,128)}, u32[]{:S(2)}) copy-start(f32[16,1024]{1,0:T(8,128)} %copy-done.10) | copy-start | bytes 196612
  362.3 12.2 %all-to-all-start.6 = ((f32[2,1,1,4,2,4,1,1024]{7,4,5,0,6,2,1,3:T(2,128)}), f32[2,1,1,4,2,4,1,1024]{7,4,5,0,6,2,1,3:T(2,128)S(1)}, u32[]{:S(2)}, u32[]{:S(2)}) async-start(f32[2,1,1,4,2,4,1,1024]{7,4,5,0,6,2,1,3:T(2,128)} %copy.130), calls=%async_computation.6 | async-start | bytes 524288 | tf_op jit(solution)/shard_map/all_to_all | solution.py:149
  432.0 19.2 %copy-start.3 = (s32[16384]{0:T(1024)S(1)}, s32[16384]{0:T(1024)}, u32[]{:S(2)}) copy-start(s32[16384]{0:T(1024)} %copy-done.2) | copy-start | bytes 196612
  432.1 19.2 %copy-start.7 = (f32[2,16384]{1,0:T(2,128)S(1)}, f32[2,16384]{1,0:T(2,128)}, u32[]{:S(2)}) copy-start(f32[2,16384]{1,0:T(2,128)} %param.9) | copy-start | bytes 393220
  432.1 19.1 %copy-start.16 = (s32[2]{0:T(128)S(1)}, s32[2]{0:T(128)}, u32[]{:S(2)}) copy-start(s32[2]{0:T(128)} %get-tuple-element.47) | copy-start | bytes 28
  432.1 19.1 %copy-start.17 = (f32[2]{0:T(128)S(1)}, f32[2]{0:T(128)}, u32[]{:S(2)}) copy-start(f32[2]{0:T(128)} %get-tuple-element.45) | copy-start | bytes 28
where the time goes:
time: 579 us; the launch traced here: 572 us
  matrix products  342 us (59%)
  blocking collectives  70.2 us (12%)
  local copies, waits for them, and re-layouts  64.4 us (11%)
  waiting for transfers between devices  56.5 us (10%)
  starting transfers between devices  17.1 us (3%)
  other arithmetic  12.7 us (2%)
  between operations  8.9 us (2%)
    dot_general x16, matrix products, complex_einsum(): imag_out = jnp.einsum(formula, data_real, table_imag, precision=exact_mode)  86.3 us
    dot_general x15, matrix products, complex_einsum(): jnp.einsum(formula, data_imag, table_imag, precision=exact_mode)  86.3 us
    dot_general x16, matrix products, complex_einsum(): real_out = jnp.einsum(formula, data_real, table_real, precision=exact_mode)  85.9 us
    dot_general x15, matrix products, complex_einsum(): jnp.einsum(formula, data_imag, table_real, precision=exact_mode)  83.7 us
    all_to_all x1, waiting for transfers between devices, to_space(): lax.all_to_all(lax.all_to_all(shaped, 'rows', split_axis=5, concat_axis=2...  31 us
    all_to_all x2, blocking collectives, to_space(): lax.all_to_all(shaped, 'rows', split_axis=5, concat_axis=2, tiled=True)  28.1 us
    unnamed x51, local copies, waits for them, and re-layouts  26.6 us
    all_to_all x2, blocking collectives, to_frequency(): lax.all_to_all(shaped, 'rows', split_axis=2, concat_axis=5, tiled=True)  22.4 us
  transfers between devices with their start and end apart: 4, of which 4 were waited for; matrix products, arithmetic and copies ran while one was open for 1% of the time, Pallas kernels for 0%

commit v1 on v0

--- a/solution.py
+++ b/solution.py
@@ -2,10 +2,500 @@
 
 import jax
 import jax.numpy as jnp
+import numpy as np
 from jax import lax
+from jax.experimental import pallas as pl
+from jax.experimental.pallas import tpu as pltpu
 from jax.sharding import PartitionSpec as P
 
-NC = 16384
+LANES = 128
+SUBLANES = 8
+
+
+def high_low(table):
+    single = jnp.asarray(table, jnp.float32)
+    high = single.astype(jnp.bfloat16)
+    low = (single - high.astype(jnp.float32)).astype(jnp.bfloat16)
+    return high, low
+
+
+def host_split(table):
+    import ml_dtypes
+
+    single = np.asarray(table, np.float32)
+    high = single.astype(ml_dtypes.bfloat16)
+    low = (single - high.astype(np.float32)).astype(ml_dtypes.bfloat16)
+    return np.stack([high, low])
+
+
+def unit_circle(left, right, period):
+    angles = 2.0 * math.pi / period * (np.outer(left, right) % period)
+    return np.cos(angles), np.sin(angles)
+
+
+def slab_rows(outer, groups, rows_count, fields_count):
+    per_source = outer // groups
+    source = np.arange(groups)
+    block = (source % fields_count) * rows_count + source // fields_count
+    return (block[:, None] * per_source + np.arange(per_source)[None, :]).reshape(-1)
+
+
+def transform_tables(total, scale, groups, rows_count, fields_count):
+    outer = total // LANES
+    x1 = slab_rows(outer, groups, rows_count, fields_count)
+    k1 = np.arange(outer)
+    x2 = np.arange(LANES)
+    first_cos, first_sin = unit_circle(k1, x1, outer)
+    last_cos, last_sin = unit_circle(x2, x2, LANES)
+    turn_cos, turn_sin = unit_circle(k1, x2, total)
+    forward_left = host_split(np.block([[first_cos, first_sin], [-first_sin, first_cos]]))
+    forward_right = host_split(np.block([[last_cos, -last_sin], [last_sin, last_cos]]))
+    inverse_right = host_split(np.block([[last_cos, last_sin], [-last_sin, last_cos]]))
+    inverse_left = host_split(
+        np.block([[first_cos.T, -first_sin.T], [first_sin.T, first_cos.T]])
+    )
+    turns = np.stack([turn_cos, -turn_sin, turn_cos * scale, turn_sin * scale])
+    return forward_left, forward_right, inverse_right, inverse_left, np.asarray(turns, np.float32)
+
+
+def rotate(cosine, sine, real, imag):
+    if imag is None:
+        return real * cosine, real * sine
+    if abs(cosine - abs(sine)) < 1e-12 or abs(cosine + abs(sine)) < 1e-12:
+        sign = 1.0 if cosine * sine > 0 else -1.0
+        if sign > 0:
+            return (real - imag) * cosine, (real + imag) * cosine
+        return (real + imag) * cosine, (imag - real) * cosine
+    return real * cosine - imag * sine, real * sine + imag * cosine
+
+
+def tile_transform(values, direction):
+    length = len(values)
+    if length == 1:
+        return values
+    even = tile_transform(values[0::2], direction)
+    odd = tile_transform(values[1::2], direction)
+    half = length // 2
+    low, high = [None] * half, [None] * half
+    for index in range(half):
+        even_real, even_imag = even[index]
+        odd_real, odd_imag = odd[index]
+        if index == 0:
+            low[0] = (
+                even_real + odd_real,
+                None if even_imag is None else even_imag + odd_imag,
+            )
+            high[0] = (
+                even_real - odd_real,
+                None if even_imag is None else even_imag - odd_imag,
+            )
+            continue
+        if 4 * index == length:
+            if odd_imag is None:
+                turned_real, turned_imag = None, odd_real
+            else:
+                turned_real, turned_imag = odd_imag, odd_real
+            if direction > 0:
+                real_low = even_real if turned_real is None else even_real - turned_real
+                real_high = even_real if turned_real is None else even_real + turned_real
+                imag_low = turned_imag if even_imag is None else even_imag + turned_imag
+                imag_high = -turned_imag if even_imag is None else even_imag - turned_imag
+            else:
+                real_low = even_real if turned_real is None else even_real + turned_real
+                real_high = even_real if turned_real is None else even_real - turned_real
+                imag_low = -turned_imag if even_imag is None else even_imag - turned_imag
+                imag_high = turned_imag if even_imag is None else even_imag + turned_imag
+            low[index] = (real_low, imag_low)
+            high[index] = (real_high, imag_high)
+            continue
+        angle = direction * 2.0 * math.pi * index / length
+        turned_real, turned_imag = rotate(math.cos(angle), math.sin(angle), odd_real, odd_imag)
+        low[index] = (
+            even_real + turned_real,
+            turned_imag if even_imag is None else even_imag + turned_imag,
+        )
+        high[index] = (
+            even_real - turned_real,
+            -turned_imag if even_imag is None else even_imag - turned_imag,
+        )
+    return low + high
+
+
+def split_product_left(table_ref, data):
+    high = data.astype(jnp.bfloat16)
+    low = (data - high.astype(jnp.float32)).astype(jnp.bfloat16)
+    product = lambda a, b: jnp.dot(a, b, preferred_element_type=jnp.float32)
+    return product(table_ref[0], high) + product(table_ref[0], low) + product(table_ref[1], high)
+
+
+def split_product_right(data, table_ref):
+    high = data.astype(jnp.bfloat16)
+    low = (data - high.astype(jnp.float32)).astype(jnp.bfloat16)
+    product = lambda a, b: jnp.dot(a, b, preferred_element_type=jnp.float32)
+    return product(high, table_ref[0]) + product(low, table_ref[0]) + product(high, table_ref[1])
+
+
+def forward_rows(pairs, left_ref, right_ref, turn_ref):
+    outer = pairs[0][0].shape[0]
+    stacked = jnp.concatenate(
+        [
+            jnp.concatenate([pair[0] for pair in pairs], axis=1),
+            jnp.concatenate([pair[1] for pair in pairs], axis=1),
+        ],
+        axis=0,
+    )
+    middle = split_product_left(left_ref, stacked)
+    cosine, sine = turn_ref[0], turn_ref[1]
+    rows = []
+    for index in range(len(pairs)):
+        real = middle[:outer, index * LANES : (index + 1) * LANES]
+        imag = middle[outer:, index * LANES : (index + 1) * LANES]
+        rows.append(
+            jnp.concatenate([real * cosine - imag * sine, real * sine + imag * cosine], axis=1)
+        )
+    result = split_product_right(jnp.concatenate(rows, axis=0), right_ref)
+    return [
+        (
+            result[index * outer : (index + 1) * outer, :LANES],
+            result[index * outer : (index + 1) * outer, LANES:],
+        )
+        for index in range(len(pairs))
+    ]
+
+
+def inverse_rows(pairs, right_ref, left_ref, turn_ref):
+    outer = pairs[0][0].shape[0]
+    stacked = jnp.concatenate([jnp.concatenate(pair, axis=1) for pair in pairs], axis=0)
+    middle = split_product_right(stacked, right_ref)
+    cosine, sine = turn_ref[2], turn_ref[3]
+    reals, imags = [], []
+    for index in range(len(pairs)):
+        real = middle[index * outer : (index + 1) * outer, :LANES]
+        imag = middle[index * outer : (index + 1) * outer, LANES:]
+        reals.append(real * cosine - imag * sine)
+        imags.append(real * sine + imag * cosine)
+    stacked = jnp.concatenate(
+        [jnp.concatenate(reals, axis=1), jnp.concatenate(imags, axis=1)], axis=0
+    )
+    result = split_product_left(left_ref, stacked)
+    return [
+        (
+            result[:outer, index * LANES : (index + 1) * LANES],
+            result[outer:, index * LANES : (index + 1) * LANES],
+        )
+        for index in range(len(pairs))
+    ]
+
+
+def split_columns_kernel(sky_ref, out_ref):
+    parts = out_ref.shape[0]
+    fields, _, width = sky_ref.shape
+    tiles = width // parts // LANES
+    for part in range(parts):
+        for field in range(fields):
+            for tile in range(tiles):
+                start = (part * tiles + tile) * LANES
+                place = (field * tiles + tile) * SUBLANES
+                out_ref[part, place : place + SUBLANES, :] = sky_ref[field, :, start : start + LANES]
+
+
+def join_columns_kernel(in_ref, out_ref):
+    parts = in_ref.shape[0]
+    fields, _, width = out_ref.shape
+    tiles = width // parts // LANES
+    for part in range(parts):
+        for field in range(fields):
+            for tile in range(tiles):
+                start = (part * tiles + tile) * LANES
+                place = (field * tiles + tile) * SUBLANES
+                out_ref[field, :, start : start + LANES] = in_ref[part, place : place + SUBLANES, :]
+
+
+def slab_forward_kernel(local_rows, sky_ref, out_ref):
+    parts, height, _ = sky_ref.shape
+    fields = height // (SUBLANES * SUBLANES)
+    for field in range(fields):
+        values = []
+        for part in range(parts):
+            for row in range(SUBLANES):
+                start = field * SUBLANES * SUBLANES + row
+                values.append(
+                    (sky_ref[part, pl.ds(start, SUBLANES, stride=SUBLANES), :], None)
+                )
+        for freq, pair in enumerate(tile_transform(values, -1.0)):
+            owner, row = divmod(freq, local_rows)
+            for side in range(2):
+                place = ((field * 2 + side) * local_rows + row) * SUBLANES
+                value = pair[side]
+                if value is None:
+                    value = jnp.zeros_like(pair[0])
+                out_ref[owner, place : place + SUBLANES, :] = value
+
+
+def tile_rows(ref, leg, local_rows):
+    values = []
+    for owner in range(ref.shape[0]):
+        for row in range(local_rows):
+            places = [((leg * 2 + side) * local_rows + row) * SUBLANES for side in range(2)]
+            values.append(tuple(ref[owner, p : p + SUBLANES, :] for p in places))
+    return values
+
+
+def product_kernel(local_rows, legs_ref, out_ref, pol_ref, sum_ref):
+    temp = tile_transform(tile_rows(legs_ref, 0, local_rows), 1.0)
+    for index, (real, imag) in enumerate(temp):
+        pol_ref[index, 0] = real
+        pol_ref[index, 1] = imag
+    grad = tile_transform(tile_rows(legs_ref, 1, local_rows), 1.0)
+    for index, (real, imag) in enumerate(grad):
+        first, second = pol_ref[index, 0], pol_ref[index, 1]
+        sum_ref[index, 0] = first * real - second * imag
+        sum_ref[index, 1] = first * imag + second * real
+    pol = tile_transform(tile_rows(legs_ref, 2, local_rows), 1.0)
+    for index, (real, imag) in enumerate(pol):
+        pol_ref[index, 0] = real * 0.5
+        pol_ref[index, 1] = imag * 0.5
+    three = tile_transform(tile_rows(legs_ref, 3, local_rows), 1.0)
+    for index, (real, imag) in enumerate(three):
+        first, second = pol_ref[index, 0], pol_ref[index, 1]
+        sum_ref[index, 0] += first * real + second * imag
+        sum_ref[index, 1] += first * imag - second * real
+    one = tile_transform(tile_rows(legs_ref, 4, local_rows), 1.0)
+    current = []
+    for index, (real, imag) in enumerate(one):
+        first, second = pol_ref[index, 0], pol_ref[index, 1]
+        current.append(
+            (
+                sum_ref[index, 0] + (first * real + second * imag),
+                sum_ref[index, 1] + (second * real - first * imag),
+            )
+        )
+    for freq, pair in enumerate(tile_transform(current, -1.0)):
+        owner, row = divmod(freq, local_rows)
+        for side in range(2):
+            place = (side * local_rows + row) * SUBLANES
+            out_ref[owner, place : place + SUBLANES, :] = pair[side]
+
+
+def slab_inverse_kernel(local_rows, in_ref, out_ref):
+    result = tile_transform(tile_rows(in_ref, 0, local_rows), 1.0)
+    for row, pair in enumerate(result):
+        part, inner = divmod(row, SUBLANES)
+        for side in range(2):
+            start = side * SUBLANES * SUBLANES + inner
+            out_ref[part, pl.ds(start, SUBLANES, stride=SUBLANES), :] = pair[side]
+
+
+def gathered_matrix(ref, place):
+    sources = ref.shape[0]
+    return ref[:, place : place + SUBLANES, :].reshape(sources * SUBLANES, LANES)
+
+
+def frequencies(row_id, outer, total, total_rows):
+    column = lax.broadcasted_iota(jnp.int32, (outer, LANES), 0) + outer * lax.broadcasted_iota(
+        jnp.int32, (outer, LANES), 1
+    )
+    freq_col = jnp.where(column < total // 2, column, column - total)
+    freq_row = jnp.where(row_id < total_rows // 2, row_id, row_id - total_rows)
+    return freq_col, freq_row
+
+
+def legs_kernel(
+    config, cuts_ref, spectra_ref, filters_ref, wiener_ref, fl_ref, fr_ref, ir_ref, il_ref, turn_ref, out_ref
+):
+    local_rows, total, total_rows = config
+    outer = total // LANES
+    ratio = total // total_rows
+    device = cuts_ref[6]
+    for row in range(local_rows):
+        pairs = []
+        for field in range(3):
+            pairs.append(
+                tuple(
+                    gathered_matrix(spectra_ref, ((field * 2 + side) * local_rows + row) * SUBLANES)
+                    for side in range(2)
+                )
+            )
+        temp, stokes_q, stokes_u = forward_rows(pairs, fl_ref, fr_ref, turn_ref)
+        freq_col, freq_row = frequencies(device * local_rows + row, outer, total, total_rows)
+        scaled = freq_row * ratio
+        square = freq_col * freq_col
+        radius = square + scaled * scaled
+        floor = jnp.maximum(radius, 1).astype(jnp.float32)
+        cosine = (square - scaled * scaled).astype(jnp.float32) / floor
+        sine = (freq_col * (2 * scaled)).astype(jnp.float32) / floor
+        along_x = freq_col.astype(jnp.float32) * (2.0 / total)
+        along_y = freq_row.astype(jnp.float32) * (2.0 / total_rows)
+
+        def weight(ref, index):
+            return ref[index, pl.ds(row, outer, stride=local_rows), :].T
+
+        def masked(lower, upper, value):
+            low, high = cuts_ref[lower], cuts_ref[upper]
+            inside = (radius >= low * low) & (radius <= high * high)
+            return jnp.where(inside, value, 0.0)
+
+        temp_weight = masked(0, 1, weight(filters_ref, 0))
+        e_weight = masked(2, 3, weight(filters_ref, 1))
+        b_weight = masked(2, 3, weight(filters_ref, 2))
+        temp_bar = (temp_weight * temp[0], temp_weight * temp[1])
+        minus_e = tuple(
+            e_weight * (cosine * stokes_q[side] + sine * stokes_u[side]) for side in range(2)
+        )
+        b_bar = tuple(
+            b_weight * (sine * stokes_q[side] - cosine * stokes_u[side]) for side in range(2)
+        )
+        wiener_temp = weight(wiener_ref, 0)
+        grad = (wiener_temp * temp_bar[0], wiener_temp * temp_bar[1])
+        grad_leg = (
+            -(along_y * grad[0]) - along_x * grad[1],
+            along_x * grad[0] - along_y * grad[1],
+        )
+        pol = (minus_e[0] + b_bar[1], minus_e[1] - b_bar[0])
+        pol_leg = (pol[0] * cosine - pol[1] * sine, pol[0] * sine + pol[1] * cosine)
+        wiener_pol = weight(wiener_ref, 1)
+        scaled_e = (wiener_pol * minus_e[0], wiener_pol * minus_e[1])
+        spin = (
+            scaled_e[0] * cosine - scaled_e[1] * sine,
+            scaled_e[0] * sine + scaled_e[1] * cosine,
+        )
+        across = (-(along_x * spin[1]), along_x * spin[0])
+        upward = (along_y * spin[0], along_y * spin[1])
+        three_leg = (across[0] - upward[0], across[1] - upward[1])
+        one_leg = (across[0] + upward[0], across[1] + upward[1])
+        legs = inverse_rows(
+            [temp_bar, grad_leg, pol_leg, three_leg, one_leg], ir_ref, il_ref, turn_ref
+        )
+        for leg, pair in enumerate(legs):
+            for side in range(2):
+                place = ((leg * 2 + side) * local_rows + row) * SUBLANES
+                out_ref[:, place : place + SUBLANES, :] = pair[side].reshape(
+                    out_ref.shape[0], SUBLANES, LANES
+                )
+
+
+def estimate_kernel(
+    config, cuts_ref, spectra_ref, response_ref, fl_ref, fr_ref, ir_ref, il_ref, turn_ref, out_ref
+):
+    local_rows, total, total_rows = config
+    outer = total // LANES
+    ratio = total // total_rows
+    device = cuts_ref[6]
+    pairs = [
+        tuple(
+            gathered_matrix(spectra_ref, (side * local_rows + row) * SUBLANES) for side in range(2)
+        )
+        for row in range(local_rows)
+    ]
+    modes = forward_rows(pairs, fl_ref, fr_ref, turn_ref)
+    estimates = []
+    for row in range(local_rows):
+        freq_col, freq_row = frequencies(device * local_rows + row, outer, total, total_rows)
+        scaled = freq_row * ratio
+        radius = freq_col * freq_col + scaled * scaled
+        low, high = cuts_ref[4], cuts_ref[5]
+        inside = (radius >= low * low) & (radius <= high * high)
+        weight = jnp.where(inside, response_ref[pl.ds(row, outer, stride=local_rows), :].T, 0.0)
+        along_x = freq_col.astype(jnp.float32) * (2.0 / total)
+        along_y = freq_row.astype(jnp.float32) * (2.0 / total_rows)
+        real, imag = weight * modes[row][0], weight * modes[row][1]
+        estimates.append(
+            (along_y * real - along_x * imag, along_y * imag + along_x * real)
+        )
+    result = inverse_rows(estimates, ir_ref, il_ref, turn_ref)
+    for row in range(local_rows):
+        for side in range(2):
+            place = (side * local_rows + row) * SUBLANES
+            out_ref[:, place : place + SUBLANES, :] = result[row][side].reshape(
+                out_ref.shape[0], SUBLANES, LANES
+            )
+
+
+def in_vmem(count):
+    return [pl.BlockSpec(memory_space=pltpu.VMEM)] * count
+
+
+def run(kernel, shape, *operands, scalars=0, scratch=()):
+    specs = [pl.BlockSpec(memory_space=pltpu.SMEM)] * scalars + in_vmem(len(operands) - scalars)
+    return pl.pallas_call(
+        kernel,
+        out_shape=jax.ShapeDtypeStruct(shape, jnp.float32),
+        in_specs=specs,
+        out_specs=pl.BlockSpec(memory_space=pltpu.VMEM),
+        scratch_shapes=list(scratch),
+        compiler_params=pltpu.CompilerParams(vmem_limit_bytes=48 * 1024 * 1024),
+    )(*operands)
+
+
+def lane_view(table, outer, local_rows):
+    lead = table.shape[:-2]
+    shaped = table.reshape(lead + (local_rows, outer, LANES))
+    order = tuple(range(len(lead))) + (len(lead) + 1, len(lead), len(lead) + 2)
+    return shaped.transpose(order).reshape(lead + (outer * local_rows, LANES))
+
+
+def tiled_body(sky_maps, band_cuts, filters, wiener, response):
+    rows_count = lax.axis_size("rows")
+    fields_count = lax.axis_size("fields")
+    both = ("rows", "fields")
+    groups = rows_count * fields_count
+    local_rows, total = filters.shape[1:]
+    total_rows = local_rows * groups
+    outer = total // LANES
+    config = (local_rows, total, total_rows)
+    scale = 1.0 / (total * total_rows)
+    tables = transform_tables(total, scale, groups, rows_count, fields_count)
+    device = lax.axis_index(both).astype(jnp.int32)
+    cuts = jnp.concatenate([band_cuts, device[None]])
+    square = SUBLANES * SUBLANES
+
+    def exchange(value, axes):
+        return lax.all_to_all(value, axes, 0, 0, tiled=True)
+
+    pieces = run(split_columns_kernel, (rows_count, 3 * square, LANES), sky_maps)
+    slabs = exchange(pieces, "rows")
+    spectra = run(
+        lambda *refs: slab_forward_kernel(local_rows, *refs),
+        (groups, 6 * local_rows * SUBLANES, LANES),
+        slabs,
+    )
+    spectra = exchange(spectra, both)
+    legs = run(
+        lambda *refs: legs_kernel(config, *refs),
+        (groups, 10 * local_rows * SUBLANES, LANES),
+        cuts,
+        spectra,
+        lane_view(filters, outer, local_rows),
+        lane_view(wiener, outer, local_rows),
+        *tables,
+        scalars=1,
+    )
+    legs = exchange(legs, both)
+    holder = pltpu.VMEM((total_rows, 2, SUBLANES, LANES), jnp.float32)
+    current = run(
+        lambda *refs: product_kernel(local_rows, *refs),
+        (groups, 2 * local_rows * SUBLANES, LANES),
+        legs,
+        scratch=(holder, holder),
+    )
+    current = exchange(current, both)
+    estimate = run(
+        lambda *refs: estimate_kernel(config, *refs),
+        (groups, 2 * local_rows * SUBLANES, LANES),
+        cuts,
+        current,
+        lane_view(response, outer, local_rows),
+        *tables,
+        scalars=1,
+    )
+    estimate = exchange(estimate, both)
+    maps = run(
+        lambda *refs: slab_inverse_kernel(local_rows, *refs),
+        (rows_count, 2 * square, LANES),
+        estimate,
+    )
+    maps = exchange(maps, "rows")
+    return run(join_columns_kernel, (2, SUBLANES, sky_maps.shape[2]), maps)
 
 
 exact_mode = lax.Precision.HIGHEST
@@ -123,18 +613,19 @@
     )
 
 
-def body(sky_maps, band_cuts, filters, wiener, response):
+def general_body(sky_maps, band_cuts, filters, wiener, response):
     rows_count = lax.axis_size("rows")
     fields_count = lax.axis_size("fields")
     groups = rows_count * fields_count
     local_rows = filters.shape[1]
     total_rows = local_rows * groups
+    NC = filters.shape[2]
     row_ratio = NC // total_rows
 
     def forward_columns(stacked):
         return jnp.stack(column_forward((stacked[0], stacked[1]), groups, fields_count))
 
-    def inverse_rows(stacked):
+    def inverse_slabs(stacked):
         return jnp.stack(row_transform((stacked[0], stacked[1]), 1.0))
 
     def inverse_columns(stacked):
@@ -169,7 +660,7 @@
             concat_axis=3,
             tiled=True,
         )
-        result = inverse_rows(arrived.reshape(2, batch_len, total_rows, block_width))
+        result = inverse_slabs(arrived.reshape(2, batch_len, total_rows, block_width))
         return result
 
     slab_spectra = jnp.stack(
@@ -257,6 +748,19 @@
     return lax.all_to_all(slab_result, "rows", split_axis=1, concat_axis=2, tiled=True)
 
 
+def fits_tiles(sky_maps, band_cuts, filters, wiener, response):
+    groups = lax.axis_size("rows") * lax.axis_size("fields")
+    return (
+        sky_maps.shape[1] == SUBLANES
+        and filters.shape[2] // groups == SUBLANES * LANES
+        and filters.shape[2] == LANES * LANES
+    )
+
+
+def body(*operands):
+    return tiled_body(*operands) if fits_tiles(*operands) else general_body(*operands)
+
+
 def solution(mesh):
     placed = (
         P("sims", "rows", "fields"),

time: 579 us -> 118 us (0.20); the launches traced: 572 us -> 117 us
  matrix products: 342 us -> 0 us
  local copies, waits for them, and re-layouts: 64.4 us -> 1.04 us
  waiting for transfers between devices: 56.5 us -> 21.1 us
  other arithmetic: 12.7 us -> 0.08 us
  starting transfers between devices: 17.1 us -> 4.98 us
  blocking collectives: 70.2 us -> 81.7 us
  between operations: 8.9 us -> 0.12 us
  Pallas kernels: 0 us -> 8.33 us
    dot_general x62 -> x0, matrix products: 342 us -> none  [the longest x16 86.3 us: complex_einsum(): imag_out = jnp.einsum(formula, data_real, table_imag, precision=exact_mode)]
    all_to_all x4 -> x1, waiting for transfers between devices: 56.5 us -> 21.1 us  [exchange(): return lax.all_to_all(value, axes, 0, 0, tiled=True)]
    unnamed x51 -> x20, local copies, waits for them, and re-layouts: 26.6 us -> 1.04 us
    another operation x40 -> x0, local copies, waits for them, and re-layouts: 16.7 us -> none  [the longest x11 5 us: body(): jnp.stack([temp_bar[0], grad_temp[0], pol_bar[0], spin_three[0], spin_one...]
    all_to_all x7 -> x0, local copies, waits for them, and re-layouts: 12.1 us -> none  [the longest x2 7.45 us: body(): lax.all_to_all(sky_maps, 'rows', split_axis=2, concat_axis=1, tiled=True)]
    all_to_all x4 -> x1, starting transfers between devices: 17.1 us -> 4.98 us  [exchange(): return lax.all_to_all(value, axes, 0, 0, tiled=True)]
    all_to_all x6 -> x5, blocking collectives: 70.2 us -> 81.7 us  [exchange(): return lax.all_to_all(value, axes, 0, 0, tiled=True)]
    pallas_call x0 -> x7, Pallas kernels: none -> 8.33 us  [run(): pl.pallas_call(kernel, out_shape=jax.ShapeDtypeStruct(shape, jnp.float32)...]
  transfers between devices with their start and end apart: 4 -> 1, of which waited for: 4 -> 1; matrix products, arithmetic and copies ran while one was open for 1% -> 0% of each run, Pallas kernels for 0% -> 0%
where the time goes in v1:
time: 118 us; the launch traced here: 117 us
  blocking collectives  81.7 us (69%)
  waiting for transfers between devices  21.1 us (18%)
  Pallas kernels  8.33 us (7%)
  starting transfers between devices  4.98 us (4%)
    all_to_all x5, blocking collectives, exchange(): return lax.all_to_all(value, axes, 0, 0, tiled=True)  81.7 us
    all_to_all x1, waiting for transfers between devices, exchange(): return lax.all_to_all(value, axes, 0, 0, tiled=True)  21.1 us
    pallas_call x7, Pallas kernels, run(): pl.pallas_call(kernel, out_shape=jax.ShapeDtypeStruct(shape, jnp.float32)...  8.33 us
    all_to_all x1, starting transfers between devices, exchange(): return lax.all_to_all(value, axes, 0, 0, tiled=True)  4.98 us
  transfers between devices with their start and end apart: 1, of which 1 were waited for; matrix products, arithmetic and copies ran while one was open for 0% of the time, Pallas kernels for 0%

profile of v1, /device:TPU:0, one launch (start us, length us, event | category | flops | bytes accessed | tf_op | source)
XLA Modules:
  0.0 117.4 jit_solution(621641240150947168)
XLA Ops:
  0.0 0.0 copy-start.6
  0.0 1.0 copy-done.6
  1.0 11.5 %all_to_all.30.refs_0_ = f32[4,192,128]{2,1,0:T(8,128)S(1)} all-to-all(f32[4,192,128]{2,1,0:T(8,128)S(1)} %shard_map.100), channel_id=1, replica_groups=mesh['sims'=2,'rows'=4,'fields'=4] {'rows'}, dimensions={0} | all-to-all | bytes 786432 | tf_op jit(solution)/shard_map/all_to_all | solution.py:453
  12.5 0.0 copy-start
  12.5 0.0 copy-start.1
  12.5 0.0 copy-start.2
  12.5 0.0 copy-start.3
  12.5 0.0 copy-start.4
  12.5 0.0 copy-start.5
  12.6 0.0 copy-start.7
  12.6 1.1 shard_map.101
  13.7 5.0 %all-to-all-start.1 = ((f32[16,96,128]{2,1,0:T(8,128)}), f32[16,96,128]{2,1,0:T(8,128)S(1)}, u32[]{:S(2)}, u32[]{:S(2)}) async-start(f32[16,96,128]{2,1,0:T(8,128)} %shard_map.101), calls=%async_computation.1 | async-start | bytes 1572864 | tf_op jit(solution)/shard_map/all_to_all | solution.py:453
  18.7 0.0 copy-done.9
  18.7 0.1 pad_add_fusion.refs_0_
  18.8 21.1 %all-to-all-done.1.refs_1_ = f32[16,96,128]{2,1,0:T(8,128)S(1)} async-done(((f32[16,96,128]{2,1,0:T(8,128)}), f32[16,96,128]{2,1,0:T(8,128)S(1)}, u32[]{:S(2)}, u32[]{:S(2)}) %all-to-all-start.1) | async-done | bytes 786464 | tf_op jit(solution)/shard_map/all_to_all | solution.py:453
  39.9 0.0 copy-done
  39.9 0.0 copy-done.1
  39.9 0.0 copy-done.2
  39.9 0.0 copy-done.3
  39.9 0.0 copy-done.4
  39.9 0.0 copy-done.5
  39.9 0.0 copy-done.7
  39.9 4.0 %shard_map.102 = f32[16,160,128]{2,1,0:T(8,128)S(1)} custom-call(s32[7]{0:T(128)S(1)} %pad_add_fusion.refs_0_, f32[16,96,128]{2,1,0:T(8,128)S(1)} %all-to-all-done.1.refs_1_, f32[3,256,128]{2,1,0:T(8,128)S(1)} %bitcast.16, f32[2,256,128]{2,1,0:T(8,128)S(1)} %bitcast.17, bf16[2,256,256]{2,1,0:T(8,128)(2,1)S(1)} %copy-done.4, ...), custom_call_target="tpu_custom_call" | custom-call | tf_op jit(solution)/shard_map/pallas_call | solution.py:420
  44.0 35.7 %all_to_all.31.refs_0_ = f32[16,160,128]{2,1,0:T(8,128)S(1)} all-to-all(f32[16,160,128]{2,1,0:T(8,128)S(1)} %shard_map.102), channel_id=1, replica_groups=mesh['sims'=2,'rows'=4,'fields'=4] {'rows','fields'}, dimensions={0} | all-to-all | bytes 2621440 | tf_op jit(solution)/shard_map/all_to_all | solution.py:453
  79.6 0.6 shard_map.103
  80.2 13.0 %all_to_all.32.refs_1_ = f32[16,32,128]{2,1,0:T(8,128)S(1)} all-to-all(f32[16,32,128]{2,1,0:T(8,128)S(1)} %shard_map.103), channel_id=1, replica_groups=mesh['sims'=2,'rows'=4,'fields'=4] {'rows','fields'}, dimensions={0} | all-to-all | bytes 524288 | tf_op jit(solution)/shard_map/all_to_all | solution.py:453
  93.2 0.0 copy-done.8
  93.2 1.8 %shard_map.104 = f32[16,32,128]{2,1,0:T(8,128)S(1)} custom-call(s32[7]{0:T(128)S(1)} %pad_add_fusion.refs_0_, f32[16,32,128]{2,1,0:T(8,128)S(1)} %all_to_all.32.refs_1_, f32[256,128]{1,0:T(8,128)S(1)} %bitcast.18, bf16[2,256,256]{2,1,0:T(8,128)(2,1)S(1)} %copy-done.4, bf16[2,256,256]{2,1,0:T(8,128)(2,1)S(1)} %copy-done.3, ...), custom_call_target="tpu_custom_call" | custom-call | tf_op jit(solution)/shard_map/pallas_call | solution.py:420
  95.0 13.2 %all_to_all.33.refs_0_ = f32[16,32,128]{2,1,0:T(8,128)S(1)} all-to-all(f32[16,32,128]{2,1,0:T(8,128)S(1)} %shard_map.104), channel_id=1, replica_groups=mesh['sims'=2,'rows'=4,'fields'=4] {'rows','fields'}, dimensions={0} | all-to-all | bytes 524288 | tf_op jit(solution)/shard_map/all_to_all | solution.py:453
  108.2 0.1 shard_map.105
  108.3 8.4 %all_to_all.34.in_ref = f32[4,128,128]{2,1,0:T(8,128)S(1)} all-to-all(f32[4,128,128]{2,1,0:T(8,128)S(1)} %shard_map.105), channel_id=1, replica_groups=mesh['sims'=2,'rows'=4,'fields'=4] {'rows'}, dimensions={0} | all-to-all | bytes 524288 | tf_op jit(solution)/shard_map/all_to_all | solution.py:453
  116.7 0.7 shard_map.106
  (3 shorter events, 0.0 us)
Async XLA Ops:
  0.0 1.0 copy-start.6
  12.5 6.2 %copy-start.9 = (s32[6]{0:T(128)S(1)}, s32[6]{0:T(128)}, u32[]{:S(2)}) copy-start(s32[6]{0:T(128)} %param.11) | copy-start | bytes 76
  12.5 27.4 %copy-start = (f32[4,128,128]{2,1,0:T(8,128)S(1)}, f32[4,128,128]{2,1,0:T(8,128)}, u32[]{:S(2)}) copy-start(f32[4,128,128]{2,1,0:T(8,128)} %constant.23.clone.refs_8_.refs_7_) | copy-start | bytes 786436
  12.5 27.4 %copy-start.1 = (bf16[2,256,256]{2,1,0:T(8,128)(2,1)S(1)}, bf16[2,256,256]{2,1,0:T(8,128)(2,1)}, u32[]{:S(2)}) copy-start(bf16[2,256,256]{2,1,0:T(8,128)(2,1)} %constant.22.clone.refs_7_.refs_6_) | copy-start | bytes 786436
  12.5 27.4 %copy-start.2 = (bf16[2,256,256]{2,1,0:T(8,128)(2,1)S(1)}, bf16[2,256,256]{2,1,0:T(8,128)(2,1)}, u32[]{:S(2)}) copy-start(bf16[2,256,256]{2,1,0:T(8,128)(2,1)} %constant.21.clone.refs_6_.refs_5_) | copy-start | bytes 786436
  12.5 27.4 %copy-start.3 = (bf16[2,256,256]{2,1,0:T(8,128)(2,1)S(1)}, bf16[2,256,256]{2,1,0:T(8,128)(2,1)}, u32[]{:S(2)}) copy-start(bf16[2,256,256]{2,1,0:T(8,128)(2,1)} %constant.20.clone.refs_5_.refs_4_) | copy-start | bytes 786436
  12.5 27.4 %copy-start.4 = (bf16[2,256,256]{2,1,0:T(8,128)(2,1)S(1)}, bf16[2,256,256]{2,1,0:T(8,128)(2,1)}, u32[]{:S(2)}) copy-start(bf16[2,256,256]{2,1,0:T(8,128)(2,1)} %constant.19.clone.refs_4_.refs_3_) | copy-start | bytes 786436
  12.5 27.4 %copy-start.5 = (f32[3,2,16384]{2,1,0:T(2,128)S(1)}, f32[3,2,16384]{2,1,0:T(2,128)}, u32[]{:S(2)}) copy-start(f32[3,2,16384]{2,1,0:T(2,128)} %param.12) | copy-start | bytes 1179652
  12.6 27.4 %copy-start.7 = (f32[2,2,16384]{2,1,0:T(2,128)S(1)}, f32[2,2,16384]{2,1,0:T(2,128)}, u32[]{:S(2)}) copy-start(f32[2,2,16384]{2,1,0:T(2,128)} %param.13) | copy-start | bytes 786436
  13.7 26.2 %all-to-all-start.1 = ((f32[16,96,128]{2,1,0:T(8,128)}), f32[16,96,128]{2,1,0:T(8,128)S(1)}, u32[]{:S(2)}, u32[]{:S(2)}) async-start(f32[16,96,128]{2,1,0:T(8,128)} %shard_map.101), calls=%async_computation.1 | async-start | bytes 1572864 | tf_op jit(solution)/shard_map/all_to_all | solution.py:453
  79.6 13.6 %copy-start.8 = (f32[2,16384]{1,0:T(2,128)S(1)}, f32[2,16384]{1,0:T(2,128)}, u32[]{:S(2)}) copy-start(f32[2,16384]{1,0:T(2,128)} %param.14) | copy-start | bytes 393220

commit v2 on v1

--- a/solution.py
+++ b/solution.py
@@ -10,13 +10,6 @@
 
 LANES = 128
 SUBLANES = 8
-
-
-def high_low(table):
-    single = jnp.asarray(table, jnp.float32)
-    high = single.astype(jnp.bfloat16)
-    low = (single - high.astype(jnp.float32)).astype(jnp.bfloat16)
-    return high, low
 
 
 def host_split(table):
@@ -187,31 +180,37 @@
     ]
 
 
-def split_columns_kernel(sky_ref, out_ref):
-    parts = out_ref.shape[0]
+def split_columns_kernel(sky_ref, *out_refs):
+    parts = len(out_refs)
     fields, _, width = sky_ref.shape
     tiles = width // parts // LANES
-    for part in range(parts):
+    for flip in range(parts):
+        part = lax.axis_index("rows") ^ flip
         for field in range(fields):
             for tile in range(tiles):
-                start = (part * tiles + tile) * LANES
+                start = pl.multiple_of((part * tiles + tile) * LANES, LANES)
                 place = (field * tiles + tile) * SUBLANES
-                out_ref[part, place : place + SUBLANES, :] = sky_ref[field, :, start : start + LANES]
-
-
-def join_columns_kernel(in_ref, out_ref):
-    parts = in_ref.shape[0]
+                out_refs[flip][place : place + SUBLANES, :] = sky_ref[field, :, pl.ds(start, LANES)]
+
+
+def join_columns_kernel(*refs):
+    in_refs, out_ref = refs[:-1], refs[-1]
+    parts = len(in_refs)
     fields, _, width = out_ref.shape
     tiles = width // parts // LANES
-    for part in range(parts):
+    for flip in range(parts):
+        part = lax.axis_index("rows") ^ flip
         for field in range(fields):
             for tile in range(tiles):
-                start = (part * tiles + tile) * LANES
+                start = pl.multiple_of((part * tiles + tile) * LANES, LANES)
                 place = (field * tiles + tile) * SUBLANES
-                out_ref[field, :, start : start + LANES] = in_ref[part, place : place + SUBLANES, :]
-
-
-def slab_forward_kernel(local_rows, sky_ref, out_ref):
+                out_ref[field, :, pl.ds(start, LANES)] = in_refs[flip][place : place + SUBLANES, :]
+
+
+def slab_forward_kernel(local_rows, *refs):
+    piece_refs, out_ref, sky_ref = refs[:-2], refs[-2], refs[-1]
+    for flip, piece_ref in enumerate(piece_refs):
+        sky_ref[lax.axis_index("rows") ^ flip] = piece_ref[...]
     parts, height, _ = sky_ref.shape
     fields = height // (SUBLANES * SUBLANES)
     for field in range(fields):
@@ -277,13 +276,16 @@
             out_ref[owner, place : place + SUBLANES, :] = pair[side]
 
 
-def slab_inverse_kernel(local_rows, in_ref, out_ref):
+def slab_inverse_kernel(local_rows, in_ref, *refs):
+    out_refs, map_ref = refs[:-1], refs[-1]
     result = tile_transform(tile_rows(in_ref, 0, local_rows), 1.0)
     for row, pair in enumerate(result):
         part, inner = divmod(row, SUBLANES)
         for side in range(2):
             start = side * SUBLANES * SUBLANES + inner
-            out_ref[part, pl.ds(start, SUBLANES, stride=SUBLANES), :] = pair[side]
+            map_ref[part, pl.ds(start, SUBLANES, stride=SUBLANES), :] = pair[side]
+    for flip, out_ref in enumerate(out_refs):
+        out_ref[...] = map_ref[lax.axis_index("rows") ^ flip]
 
 
 def gathered_matrix(ref, place):
@@ -306,7 +308,8 @@
     local_rows, total, total_rows = config
     outer = total // LANES
     ratio = total // total_rows
-    device = cuts_ref[6]
+    device = lax.axis_index(("rows", "fields"))
+    squares = [cuts_ref[cut : cut + 1, :] * cuts_ref[cut : cut + 1, :] for cut in range(4)]
     for row in range(local_rows):
         pairs = []
         for field in range(3):
@@ -331,8 +334,7 @@
             return ref[index, pl.ds(row, outer, stride=local_rows), :].T
 
         def masked(lower, upper, value):
-            low, high = cuts_ref[lower], cuts_ref[upper]
-            inside = (radius >= low * low) & (radius <= high * high)
+            inside = (radius >= squares[lower]) & (radius <= squares[upper])
             return jnp.where(inside, value, 0.0)
 
         temp_weight = masked(0, 1, weight(filters_ref, 0))
@@ -380,7 +382,7 @@
     local_rows, total, total_rows = config
     outer = total // LANES
     ratio = total // total_rows
-    device = cuts_ref[6]
+    device = lax.axis_index(("rows", "fields"))
     pairs = [
         tuple(
             gathered_matrix(spectra_ref, (side * local_rows + row) * SUBLANES) for side in range(2)
@@ -389,12 +391,12 @@
     ]
     modes = forward_rows(pairs, fl_ref, fr_ref, turn_ref)
     estimates = []
+    squares = [cuts_ref[cut : cut + 1, :] * cuts_ref[cut : cut + 1, :] for cut in (4, 5)]
     for row in range(local_rows):
         freq_col, freq_row = frequencies(device * local_rows + row, outer, total, total_rows)
         scaled = freq_row * ratio
         radius = freq_col * freq_col + scaled * scaled
-        low, high = cuts_ref[4], cuts_ref[5]
-        inside = (radius >= low * low) & (radius <= high * high)
+        inside = (radius >= squares[0]) & (radius <= squares[1])
         weight = jnp.where(inside, response_ref[pl.ds(row, outer, stride=local_rows), :].T, 0.0)
         along_x = freq_col.astype(jnp.float32) * (2.0 / total)
         along_y = freq_row.astype(jnp.float32) * (2.0 / total_rows)
@@ -411,20 +413,25 @@
             )
 
 
-def in_vmem(count):
-    return [pl.BlockSpec(memory_space=pltpu.VMEM)] * count
-
-
-def run(kernel, shape, *operands, scalars=0, scratch=()):
-    specs = [pl.BlockSpec(memory_space=pltpu.SMEM)] * scalars + in_vmem(len(operands) - scalars)
+def run(kernel, shape, *operands, scratch=(), copies=None):
+    result = jax.ShapeDtypeStruct(shape, jnp.float32)
+    place = pl.BlockSpec(memory_space=pltpu.VMEM)
     return pl.pallas_call(
         kernel,
-        out_shape=jax.ShapeDtypeStruct(shape, jnp.float32),
-        in_specs=specs,
-        out_specs=pl.BlockSpec(memory_space=pltpu.VMEM),
+        out_shape=result if copies is None else [result] * copies,
+        in_specs=[place] * len(operands),
+        out_specs=place if copies is None else [place] * copies,
         scratch_shapes=list(scratch),
         compiler_params=pltpu.CompilerParams(vmem_limit_bytes=48 * 1024 * 1024),
     )(*operands)
+
+
+def exchange_pieces(pieces, axis):
+    count = len(pieces)
+    return [pieces[0]] + [
+        lax.ppermute(pieces[flip], axis, [(index, index ^ flip) for index in range(count)])
+        for flip in range(1, count)
+    ]
 
 
 def lane_view(table, outer, local_rows):
@@ -445,19 +452,22 @@
     config = (local_rows, total, total_rows)
     scale = 1.0 / (total * total_rows)
     tables = transform_tables(total, scale, groups, rows_count, fields_count)
-    device = lax.axis_index(both).astype(jnp.int32)
-    cuts = jnp.concatenate([band_cuts, device[None]])
+    cuts = jnp.broadcast_to(
+        jnp.pad(band_cuts, (0, SUBLANES - band_cuts.shape[0]))[:, None], (SUBLANES, LANES)
+    )
     square = SUBLANES * SUBLANES
 
     def exchange(value, axes):
         return lax.all_to_all(value, axes, 0, 0, tiled=True)
 
-    pieces = run(split_columns_kernel, (rows_count, 3 * square, LANES), sky_maps)
-    slabs = exchange(pieces, "rows")
+    pieces = run(split_columns_kernel, (3 * square, LANES), sky_maps, copies=rows_count)
+    slabs = exchange_pieces(pieces, "rows")
+    cuts, slabs = lax.optimization_barrier((cuts, slabs))
     spectra = run(
         lambda *refs: slab_forward_kernel(local_rows, *refs),
         (groups, 6 * local_rows * SUBLANES, LANES),
-        slabs,
+        *slabs,
+        scratch=(pltpu.VMEM((rows_count, 3 * square, LANES), jnp.float32),),
     )
     spectra = exchange(spectra, both)
     legs = run(
@@ -468,7 +478,6 @@
         lane_view(filters, outer, local_rows),
         lane_view(wiener, outer, local_rows),
         *tables,
-        scalars=1,
     )
     legs = exchange(legs, both)
     holder = pltpu.VMEM((total_rows, 2, SUBLANES, LANES), jnp.float32)
@@ -486,16 +495,17 @@
         current,
         lane_view(response, outer, local_rows),
         *tables,
-        scalars=1,
     )
     estimate = exchange(estimate, both)
     maps = run(
         lambda *refs: slab_inverse_kernel(local_rows, *refs),
-        (rows_count, 2 * square, LANES),
+        (2 * square, LANES),
         estimate,
-    )
-    maps = exchange(maps, "rows")
-    return run(join_columns_kernel, (2, SUBLANES, sky_maps.shape[2]), maps)
+        scratch=(pltpu.VMEM((rows_count, 2 * square, LANES), jnp.float32),),
+        copies=rows_count,
+    )
+    maps = exchange_pieces(maps, "rows")
+    return run(join_columns_kernel, (2, SUBLANES, sky_maps.shape[2]), *maps)
 
 
 exact_mode = lax.Precision.HIGHEST
@@ -754,6 +764,7 @@
         sky_maps.shape[1] == SUBLANES
         and filters.shape[2] // groups == SUBLANES * LANES
         and filters.shape[2] == LANES * LANES
+        and lax.axis_size("rows") & (lax.axis_size("rows") - 1) == 0
     )
 
 

time: 118 us -> 111 us (0.941)
  waiting for transfers between devices: 21.1 us -> 8.2 us
  blocking collectives: 81.7 us -> 88.9 us
  Pallas kernels: 8.33 us -> 6.47 us
    all_to_all x1 -> x0, waiting for transfers between devices: 21.1 us -> none  [exchange(): return lax.all_to_all(value, axes, 0, 0, tiled=True)]
    ppermute x0 -> x6, waiting for transfers between devices: none -> 8.2 us  [exchange_pieces(): lax.ppermute(pieces[flip], axis, [(index, index ^ flip) for index in rang...]
    all_to_all x5 -> x4, blocking collectives: 81.7 us -> 88.9 us  [exchange(): return lax.all_to_all(value, axes, 0, 0, tiled=True)]
    ppermute x0 -> x6, starting transfers between devices: none -> 5.1 us  [exchange_pieces(): lax.ppermute(pieces[flip], axis, [(index, index ^ flip) for index in rang...]
    all_to_all x1 -> x0, starting transfers between devices: 4.98 us -> none  [exchange(): return lax.all_to_all(value, axes, 0, 0, tiled=True)]
    pallas_call x7, Pallas kernels: 8.33 us -> 6.47 us  [run(): pl.pallas_call(kernel, out_shape=result if copies is None else [result] *...]
  transfers between devices with their start and end apart: 1 -> 6, of which waited for: 1 -> 4; matrix products, arithmetic and copies ran while one was open for 0% -> 1% of each run, Pallas kernels for 0% -> 0%
where the time goes in v2:
time: 111 us
  blocking collectives  88.9 us (80%)
  waiting for transfers between devices  8.2 us (7%)
  Pallas kernels  6.47 us (6%)
  starting transfers between devices  5.1 us (5%)
  local copies, waits for them, and re-layouts  1.76 us (2%)
    all_to_all x4, blocking collectives, exchange(): return lax.all_to_all(value, axes, 0, 0, tiled=True)  88.9 us
    ppermute x6, waiting for transfers between devices, exchange_pieces(): lax.ppermute(pieces[flip], axis, [(index, index ^ flip) for index in rang...  8.2 us
    pallas_call x7, Pallas kernels, run(): pl.pallas_call(kernel, out_shape=result if copies is None else [result] *...  6.47 us
    ppermute x6, starting transfers between devices, exchange_pieces(): lax.ppermute(pieces[flip], axis, [(index, index ^ flip) for index in rang...  5.1 us
  transfers between devices with their start and end apart: 6, of which 4 were waited for; matrix products, arithmetic and copies ran while one was open for 1% of the time, Pallas kernels for 0%

profile of v2, /device:TPU:0, one launch (start us, length us, event | category | flops | bytes accessed | tf_op | source)
XLA Modules:
  0.0 110.5 jit_solution(8312602710090269011)
XLA Ops:
  0.0 1.0 copy-done.6
  1.0 0.1 shard_map.100
  1.1 0.6 collective-permute-start
  1.6 2.6 %collective-permute-start.1 = (f32[192,128]{1,0:T(8,128)S(1)}, f32[192,128]{1,0:T(8,128)S(1)}, u32[]{:S(2)}, u32[]{:S(2)}) collective-permute-start(f32[192,128]{1,0:T(8,128)S(1)} %get-tuple-element.20), channel_id=1, source_target_pairs={{0,8},{4,12},{8,0},{12,4},{1,9},{5,13},{9,1},{13,5},{2,10},{6,14},... | collective-permute-start | bytes 294920 | tf_op jit(solution)/shard_map/ppermute | solution.py:432
  4.2 0.0 collective-permute-start.2
  4.2 0.7 pad.4
  4.9 0.0 collective-permute-done.refs_1_
  4.9 2.9 %collective-permute-done.1.refs_2_ = f32[192,128]{1,0:T(8,128)S(1)} collective-permute-done((f32[192,128]{1,0:T(8,128)S(1)}, f32[192,128]{1,0:T(8,128)S(1)}, u32[]{:S(2)}, u32[]{:S(2)}) %collective-permute-start.1) | collective-permute-done | bytes 98336 | tf_op jit(solution)/shard_map/ppermute | solution.py:432
  7.8 1.6 %collective-permute-done.2.refs_3_ = f32[192,128]{1,0:T(8,128)S(1)} collective-permute-done((f32[192,128]{1,0:T(8,128)S(1)}, f32[192,128]{1,0:T(8,128)S(1)}, u32[]{:S(2)}, u32[]{:S(2)}) %collective-permute-start.2) | collective-permute-done | bytes 98336 | tf_op jit(solution)/shard_map/ppermute | solution.py:432
  9.4 0.1 broadcast_in_dim.2.refs_0_
  9.5 0.0 copy-start.5
  9.5 0.0 copy-start.7
  9.5 0.2 shard_map.101
  9.8 27.0 %all_to_all.20.refs_1_ = f32[16,96,128]{2,1,0:T(8,128)S(1)} all-to-all(f32[16,96,128]{2,1,0:T(8,128)S(1)} %shard_map.101), channel_id=1, replica_groups=mesh['sims'=2,'rows'=4,'fields'=4] {'rows','fields'}, dimensions={0} | all-to-all | bytes 1572864 | tf_op jit(solution)/shard_map/all_to_all | solution.py:461
  36.8 0.0 copy-done
  36.8 0.0 copy-done.1
  36.8 0.0 copy-done.2
  36.9 3.5 %shard_map.102 = f32[16,160,128]{2,1,0:T(8,128)S(1)} custom-call(s32[8,128]{1,0:T(8,128)S(1)} %broadcast_in_dim.2.refs_0_, f32[16,96,128]{2,1,0:T(8,128)S(1)} %all_to_all.20.refs_1_, f32[3,256,128]{2,1,0:T(8,128)S(1)} %bitcast.15, f32[2,256,128]{2,1,0:T(8,128)S(1)} %bitcast.16, bf16[2,256,256]{2,1,0:T(8,128)(2,1)S(1)} %copy-done.4, ...), custom_call_target="tpu_custom_call" | custom-call | tf_op jit(solution)/shard_map/pallas_call | solution.py:419
  40.4 35.7 %all_to_all.21.refs_0_ = f32[16,160,128]{2,1,0:T(8,128)S(1)} all-to-all(f32[16,160,128]{2,1,0:T(8,128)S(1)} %shard_map.102), channel_id=1, replica_groups=mesh['sims'=2,'rows'=4,'fields'=4] {'rows','fields'}, dimensions={0} | all-to-all | bytes 2621440 | tf_op jit(solution)/shard_map/all_to_all | solution.py:461
  76.0 0.6 shard_map.103
  76.6 13.0 %all_to_all.22.refs_1_ = f32[16,32,128]{2,1,0:T(8,128)S(1)} all-to-all(f32[16,32,128]{2,1,0:T(8,128)S(1)} %shard_map.103), channel_id=1, replica_groups=mesh['sims'=2,'rows'=4,'fields'=4] {'rows','fields'}, dimensions={0} | all-to-all | bytes 524288 | tf_op jit(solution)/shard_map/all_to_all | solution.py:461
  89.6 0.0 copy-done.8
  89.6 1.3 %shard_map.104 = f32[16,32,128]{2,1,0:T(8,128)S(1)} custom-call(s32[8,128]{1,0:T(8,128)S(1)} %broadcast_in_dim.2.refs_0_, f32[16,32,128]{2,1,0:T(8,128)S(1)} %all_to_all.22.refs_1_, f32[256,128]{1,0:T(8,128)S(1)} %bitcast.17, bf16[2,256,256]{2,1,0:T(8,128)(2,1)S(1)} %copy-done.4, bf16[2,256,256]{2,1,0:T(8,128)(2,1)S(1)} %copy-done.3, ...), custom_call_target="tpu_custom_call" | custom-call | tf_op jit(solution)/shard_map/pallas_call | solution.py:419
  90.9 13.2 %all_to_all.23.refs_0_ = f32[16,32,128]{2,1,0:T(8,128)S(1)} all-to-all(f32[16,32,128]{2,1,0:T(8,128)S(1)} %shard_map.104), channel_id=1, replica_groups=mesh['sims'=2,'rows'=4,'fields'=4] {'rows','fields'}, dimensions={0} | all-to-all | bytes 524288 | tf_op jit(solution)/shard_map/all_to_all | solution.py:461
  104.1 0.1 shard_map.105
  104.2 0.1 collective-permute-start.3
  104.3 1.1 %collective-permute-start.4 = (f32[128,128]{1,0:T(8,128)S(1)}, f32[128,128]{1,0:T(8,128)S(1)}, u32[]{:S(2)}, u32[]{:S(2)}) collective-permute-start(f32[128,128]{1,0:T(8,128)S(1)} %get-tuple-element.29), channel_id=1, source_target_pairs={{0,8},{4,12},{8,0},{12,4},{1,9},{5,13},{9,1},{13,5},{2,10},{6,14},... | collective-permute-start | bytes 196616 | tf_op jit(solution)/shard_map/ppermute | solution.py:432
  105.4 0.7 collective-permute-start.5
  106.1 0.0 collective-permute-done.3.refs_1_
  106.1 3.0 %collective-permute-done.4.refs_2_ = f32[128,128]{1,0:T(8,128)S(1)} collective-permute-done((f32[128,128]{1,0:T(8,128)S(1)}, f32[128,128]{1,0:T(8,128)S(1)}, u32[]{:S(2)}, u32[]{:S(2)}) %collective-permute-start.4) | collective-permute-done | bytes 65568 | tf_op jit(solution)/shard_map/ppermute | solution.py:432
  109.1 0.6 collective-permute-done.5.refs_3_
  109.8 0.7 shard_map.106
  (11 shorter events, 0.0 us)
Async XLA Ops:
  0.0 1.0 copy-start.6
  1.1 3.8 %collective-permute-start = (f32[192,128]{1,0:T(8,128)S(1)}, f32[192,128]{1,0:T(8,128)S(1)}, u32[]{:S(2)}, u32[]{:S(2)}) collective-permute-start(f32[192,128]{1,0:T(8,128)S(1)} %get-tuple-element.19), channel_id=1, source_target_pairs={{0,4},{4,0},{8,12},{12,8},{1,5},{5,1},{9,13},{13,9},{2,6},{6,2},{1... | collective-permute-start | bytes 294920 | tf_op jit(solution)/shard_map/ppermute | solution.py:432
  1.6 6.2 %collective-permute-start.1 = (f32[192,128]{1,0:T(8,128)S(1)}, f32[192,128]{1,0:T(8,128)S(1)}, u32[]{:S(2)}, u32[]{:S(2)}) collective-permute-start(f32[192,128]{1,0:T(8,128)S(1)} %get-tuple-element.20), channel_id=1, source_target_pairs={{0,8},{4,12},{8,0},{12,4},{1,9},{5,13},{9,1},{13,5},{2,10},{6,14},... | collective-permute-start | bytes 294920 | tf_op jit(solution)/shard_map/ppermute | solution.py:432
  4.2 5.2 %collective-permute-start.2 = (f32[192,128]{1,0:T(8,128)S(1)}, f32[192,128]{1,0:T(8,128)S(1)}, u32[]{:S(2)}, u32[]{:S(2)}) collective-permute-start(f32[192,128]{1,0:T(8,128)S(1)} %get-tuple-element.21), channel_id=1, source_target_pairs={{0,12},{4,8},{8,4},{12,0},{1,13},{5,9},{9,5},{13,1},{2,14},{6,10},... | collective-permute-start | bytes 294920 | tf_op jit(solution)/shard_map/ppermute | solution.py:432
  9.5 27.3 %copy-start = (f32[4,128,128]{2,1,0:T(8,128)S(1)}, f32[4,128,128]{2,1,0:T(8,128)}, u32[]{:S(2)}) copy-start(f32[4,128,128]{2,1,0:T(8,128)} %constant.16.clone.refs_8_.refs_7_) | copy-start | bytes 786436
  9.5 27.3 %copy-start.1 = (bf16[2,256,256]{2,1,0:T(8,128)(2,1)S(1)}, bf16[2,256,256]{2,1,0:T(8,128)(2,1)}, u32[]{:S(2)}) copy-start(bf16[2,256,256]{2,1,0:T(8,128)(2,1)} %constant.15.clone.refs_7_.refs_6_) | copy-start | bytes 786436
  9.5 27.3 %copy-start.2 = (bf16[2,256,256]{2,1,0:T(8,128)(2,1)S(1)}, bf16[2,256,256]{2,1,0:T(8,128)(2,1)}, u32[]{:S(2)}) copy-start(bf16[2,256,256]{2,1,0:T(8,128)(2,1)} %constant.14.clone.refs_6_.refs_5_) | copy-start | bytes 786436
  9.5 27.3 %copy-start.3 = (bf16[2,256,256]{2,1,0:T(8,128)(2,1)S(1)}, bf16[2,256,256]{2,1,0:T(8,128)(2,1)}, u32[]{:S(2)}) copy-start(bf16[2,256,256]{2,1,0:T(8,128)(2,1)} %constant.13.clone.refs_5_.refs_4_) | copy-start | bytes 786436
  9.5 27.3 %copy-start.4 = (bf16[2,256,256]{2,1,0:T(8,128)(2,1)S(1)}, bf16[2,256,256]{2,1,0:T(8,128)(2,1)}, u32[]{:S(2)}) copy-start(bf16[2,256,256]{2,1,0:T(8,128)(2,1)} %constant.12.clone.refs_4_.refs_3_) | copy-start | bytes 786436
  9.5 27.3 %copy-start.5 = (f32[3,2,16384]{2,1,0:T(2,128)S(1)}, f32[3,2,16384]{2,1,0:T(2,128)}, u32[]{:S(2)}) copy-start(f32[3,2,16384]{2,1,0:T(2,128)} %param.12) | copy-start | bytes 1179652
  9.5 27.3 %copy-start.7 = (f32[2,2,16384]{2,1,0:T(2,128)S(1)}, f32[2,2,16384]{2,1,0:T(2,128)}, u32[]{:S(2)}) copy-start(f32[2,2,16384]{2,1,0:T(2,128)} %param.13) | copy-start | bytes 786436
  76.0 13.6 %copy-start.8 = (f32[2,16384]{1,0:T(2,128)S(1)}, f32[2,16384]{1,0:T(2,128)}, u32[]{:S(2)}) copy-start(f32[2,16384]{1,0:T(2,128)} %param.14) | copy-start | bytes 393220
  104.2 1.9 %collective-permute-start.3 = (f32[128,128]{1,0:T(8,128)S(1)}, f32[128,128]{1,0:T(8,128)S(1)}, u32[]{:S(2)}, u32[]{:S(2)}) collective-permute-start(f32[128,128]{1,0:T(8,128)S(1)} %get-tuple-element.28), channel_id=1, source_target_pairs={{0,4},{4,0},{8,12},{12,8},{1,5},{5,1},{9,13},{13,9},{2,6},{6,2},{1... | collective-permute-start | bytes 196616 | tf_op jit(solution)/shard_map/ppermute | solution.py:432
  104.3 4.9 %collective-permute-start.4 = (f32[128,128]{1,0:T(8,128)S(1)}, f32[128,128]{1,0:T(8,128)S(1)}, u32[]{:S(2)}, u32[]{:S(2)}) collective-permute-start(f32[128,128]{1,0:T(8,128)S(1)} %get-tuple-element.29), channel_id=1, source_target_pairs={{0,8},{4,12},{8,0},{12,4},{1,9},{5,13},{9,1},{13,5},{2,10},{6,14},... | collective-permute-start | bytes 196616 | tf_op jit(solution)/shard_map/ppermute | solution.py:432
  105.4 4.4 %collective-permute-start.5 = (f32[128,128]{1,0:T(8,128)S(1)}, f32[128,128]{1,0:T(8,128)S(1)}, u32[]{:S(2)}, u32[]{:S(2)}) collective-permute-start(f32[128,128]{1,0:T(8,128)S(1)} %get-tuple-element.30), channel_id=1, source_target_pairs={{0,12},{4,8},{8,4},{12,0},{1,13},{5,9},{9,5},{13,1},{2,14},{6,10},... | collective-permute-start | bytes 196616 | tf_op jit(solution)/shard_map/ppermute | solution.py:432
